TPU v7x, 32 devices: a whole 2x2x4 slice. The times are simulated.
32 devices in a mesh: seq: 16 (over z, y, x), head: 2 (over core).
Axes of the slice: x: 2, y: 2, z: 4, core: 2. Of those that a mesh axis runs over, the one named last changes fastest.
Arguments:
- hidden_state: bfloat16 [8, 4096], replicated, may hold values from -18 to 18
- query_weight: bfloat16 [4096, 2, 2048], P('seq', 'head'), may hold values from -1 to 1
- up_key: bfloat16 [2, 256, 512], P('head'), may hold values from -1 to 1
- up_value: bfloat16 [2, 256, 512], P('head'), may hold values from -0.375 to 0.375
- latent_key: bfloat16 [8, 16384, 2, 256], P(None, 'seq', 'head'), may hold values from -256 to 256
- latent_value: bfloat16 [8, 16384, 2, 256], P(None, 'seq', 'head'), may hold values from -6 to 6
- lengths: int32 [8], replicated, may hold values from 12288 to 16384
- block_mask: int32 [8, 64], P(None, 'seq'), may hold values from 0 to 1, as said below
- out_weight: bfloat16 [2, 2048, 4096], P('head', 'seq'), may hold values from -0.09375 to 0.09375
Outputs:
- attn_out: float32 [8, 4096], replicated
Inputs may be any that keep to these rules, and one draw needn't show every extreme that they name: `block_mask`: blocks 0 and 32 of every sequence are valid.
All inputs are finite; a program needn't handle non-finite values.
Results may differ from a plain program's by a relative error of at most 0.0035.
Values sent between devices are 32-bit elements; how exact they have to be, the bound alone decides.
No kernel may reach another device: no remote copies, remote signals or barrier semaphores. Data moves between devices by JAX's collectives and lax.ppermute only.
A program may use at most 64 MiB of HBM per device.

v0:
```python
import math
import jax
import jax.numpy as jnp
from jax import lax
from jax.sharding import PartitionSpec as P

HD = 128
R = 256
BLOCK = 256
KPG = 4
REP = 4
QW = 2048


def joined(part, axis, combine):
    gathered = jax.tree.map(lambda a: lax.all_gather(a, axis), part)

    def take(source):
        return jax.tree.map(lambda a: lax.dynamic_index_in_dim(a, source, 0, False), gathered)

    return lax.fori_loop(
        1, lax.axis_size(axis), lambda source, state: combine(state, take(source)), take(0)
    )


def join_carries(earlier, later):
    peak_a, total_a, summed_a = earlier
    peak_b, total_b, summed_b = later
    peak = jnp.maximum(peak_a, peak_b)
    factor_a = jnp.exp(peak_a - peak)
    factor_b = jnp.exp(peak_b - peak)
    total = total_a * factor_a + total_b * factor_b
    summed = summed_a * factor_a[..., None] + summed_b * factor_b[..., None]
    return (peak, total, summed)


def body(
    hidden_state,
    query_weight,
    up_key,
    up_value,
    latent_key,
    latent_value,
    lengths,
    block_mask,
    out_weight,
):
    highest = lax.Precision.HIGHEST
    seq_index = lax.axis_index("seq")
    batch = hidden_state.shape[0]
    dim_rows = query_weight.shape[0]
    state_rows = lax.dynamic_slice_in_dim(hidden_state, seq_index * dim_rows, dim_rows, 1)
    partial_query = jnp.dot(state_rows, query_weight[:, 0, :], preferred_element_type=jnp.float32)
    query = lax.psum(partial_query, "seq")
    query_heads = query.reshape(batch, KPG, REP, HD)
    keys_lat = latent_key[:, :, 0, :]
    values_lat = latent_value[:, :, 0, :]
    context_len = keys_lat.shape[1]
    positions = seq_index * context_len + jnp.arange(context_len, dtype=jnp.int32)
    block_full = jnp.repeat(block_mask, BLOCK, axis=1)
    valid = (positions[None, :] < lengths[:, None]) & (block_full > 0)
    mask_heads = valid[:, None, None, :]
    scale = 1.0 / math.sqrt(HD)
    key_maps = up_key[0].astype(jnp.float32).reshape(R, KPG, HD)
    query_latent = jnp.einsum("bjrd,ejd->bjre", query_heads, key_maps, precision=highest)
    scores = (
        jnp.einsum("bjre,bce->bjrc", query_latent, keys_lat.astype(jnp.float32), precision=highest)
        * scale
    )
    peak = jnp.max(jnp.where(mask_heads, scores, -1e30), axis=-1)
    weights = jnp.where(mask_heads, jnp.exp(scores - peak[..., None]), 0.0)
    total = jnp.sum(weights, axis=-1)
    value_maps = up_value[0].astype(jnp.float32).reshape(R, KPG, HD)
    latent_sum = jnp.einsum(
        "bjrc,bce->bjre", weights, values_lat.astype(jnp.float32), precision=highest
    )
    summed = jnp.einsum("bjre,ejd->bjrd", latent_sum, value_maps, precision=highest)
    out_rows = out_weight.shape[1]
    peak_all, total_all, summed_all = joined((peak, total, summed), "seq", join_carries)
    context = (summed_all / total_all[..., None]).reshape(batch, QW).astype(jnp.bfloat16)
    context_rows = lax.dynamic_slice_in_dim(context, seq_index * out_rows, out_rows, 1)
    partial_out = jnp.dot(context_rows, out_weight[0], preferred_element_type=jnp.float32)
    return lax.psum(partial_out, ("seq", "head"))


def solution(mesh):
    in_specs = (
        P(),
        P("seq", "head", None),
        P("head", None, None),
        P("head", None, None),
        P(None, "seq", "head", None),
        P(None, "seq", "head", None),
        P(),
        P(None, "seq"),
        P("head", "seq", None),
    )
    out_specs = P()
    return jax.shard_map(body, mesh=mesh, in_specs=in_specs, out_specs=out_specs, check_vma=False)
```

profile of v0, /device:TPU:0, one launch (start us, length us, event | category | flops | bytes accessed | tf_op | source)
XLA Modules:
  0.0 361.0 jit_solution(18013315302296954894)
XLA Ops:
  6.5 1.6 fusion.13
  8.1 0.7 copy.28
  8.8 0.7 broadcast_compare_fusion
  9.6 0.7 compare_and_fusion
  10.3 1.0 reshape.54
  11.4 1.0 reshape.55
  12.4 106.7 %all-reduce.3.cloned.1.call-done = f32[8,4,4,128]{3,2,1,0:T(4,128)} async-done(((f32[8,4,4,128]{3,2,1,0:T(4,128)}), f32[8,4,4,128]{3,2,1,0:T(4,128)}) %all-reduce.3.cloned.1.call-update) | async-done | bytes 65552 | tf_op jit(solution)/shard_map/psum | solution.py:54
  119.1 1.4 convolution_bitcast_fusion
  120.4 5.7 %select_reduce_fusion = (f32[8,4,4]{2,1,0:T(4,128)S(1)}, f32[8,4,4,1024]{3,2,1,0:T(4,128)S(1)}) fusion(pred[8,1024]{1,0:T(8,128)(4,1)S(1)} %compare_and_fusion, f32[8,4,4,256]{3,2,1,0:T(4,128)S(1)} %convolution_bitcast_fusion, bf16[8,1024,1,256]{3,1,2,0:T(8,128)(2,1)} %param.15), kind=kOutput, calls=%fused_computation.22 | convolution fusion | flops 403046272 | bytes 4858368 | tf_op jit(solution)/shard_map/bjre,bce->bjrc/dot_general | solution.py:67
  126.1 2.1 fusion.4
  128.2 0.9 convolution_bitcast_fusion.1
  129.2 40.4 %all-gather = f32[128,4,4]{2,1,0:T(4,128)S(1)} all-gather(f32[8,4,4]{2,1,0:T(4,128)S(1)} %get-tuple-element.223), channel_id=2, replica_groups=mesh['seq'=16,'head'=2] {'seq'}, dimensions={0}, use_global_device_ids=true | all-gather | bytes 8704 | tf_op jit(solution)/shard_map/all_gather | solution.py:16
  169.8 0.5 copy.37
  170.2 0.4 fusion.15
  170.6 37.1 %all-gather.1 = f32[128,4,4]{2,1,0:T(4,128)S(1)} all-gather(f32[8,4,4]{2,1,0:T(4,128)S(1)} %fusion.15), channel_id=3, replica_groups=mesh['seq'=16,'head'=2] {'seq'}, dimensions={0}, use_global_device_ids=true | all-gather | bytes 8704 | tf_op jit(solution)/shard_map/all_gather | solution.py:16
  207.9 0.5 copy.38
  208.4 0.8 slice.8
  209.2 20.1 %while.19 = (s32[]{:T(128)}, f32[8,4,4]{0,2,1:T(4,128)S(1)}, f32[8,4,4]{0,2,1:T(4,128)S(1)}, f32[8,4,4,128]{3,2,1,0:T(4,128)S(1)}, f32[16,8,4,4]{1,3,2,0:T(4,128...) while((s32[]{:T(128)}, f32[8,4,4]{0,2,1:T(4,128)S(1)}, ...), condition=%wide.region_4.5_spmd, body=%wide.region_3.4_spmd.sunk | while | flops 49925 | bytes 334991 | solution.py:21
  209.5 0.8 constant_dynamic-slice_fusion.2
  210.3 0.2 fusion.34
  210.8 0.8 constant_dynamic-slice_fusion.2
  211.7 0.2 fusion.34
  212.2 0.8 constant_dynamic-slice_fusion.2
  213.0 0.2 fusion.34
  213.5 0.8 constant_dynamic-slice_fusion.2
  214.4 0.2 fusion.34
  214.9 0.8 constant_dynamic-slice_fusion.2
  215.7 0.2 fusion.34
  216.2 0.8 constant_dynamic-slice_fusion.2
  217.0 0.2 fusion.34
  217.5 0.8 constant_dynamic-slice_fusion.2
  218.4 0.2 fusion.34
  218.9 0.8 constant_dynamic-slice_fusion.2
  219.7 0.2 fusion.34
  220.2 0.8 constant_dynamic-slice_fusion.2
  221.1 0.2 fusion.34
  221.5 0.8 constant_dynamic-slice_fusion.2
  222.9 0.8 constant_dynamic-slice_fusion.2
  224.2 0.8 constant_dynamic-slice_fusion.2
  225.1 0.2 fusion.34
  225.6 0.8 constant_dynamic-slice_fusion.2
  226.4 0.2 fusion.34
  226.9 0.8 constant_dynamic-slice_fusion.2
  228.2 0.8 constant_dynamic-slice_fusion.2
  229.1 0.2 fusion.34
  229.6 0.9 fusion.11
  230.5 122.4 %all-reduce.5.cloned.1.call-done = f32[8,4096]{1,0:T(8,128)} async-done(((f32[8,4096]{1,0:T(8,128)}), f32[8,4096]{1,0:T(8,128)}) %all-reduce.5.cloned.1.call-update) | async-done | bytes 131088 | tf_op jit(solution)/shard_map/psum | solution.py:83
  352.9 1.6 copy.84
  (69 shorter events, 5.0 us)
Async XLA Ops:
  6.5 223.1 %copy-start = (bf16[1,128,4096]{2,1,0:T(8,128)(2,1)S(1)}, bf16[1,128,4096]{2,1,0:T(8,128)(2,1)}, u32[]{:S(2)}) copy-start(bf16[1,128,4096]{2,1,0:T(8,128)(2,1)} %param.19) | copy-start | bytes 3145732
  6.5 112.5 %all-reduce.3.cloned.1.call-start = ((), (), s32[]{:S(2)}) async-start(), calls=%async_computation | async-start | bytes 131072 | tf_op jit(solution)/shard_map/psum | solution.py:54
  8.8 199.6 %all-gather.5.cloned.1.call-start = ((), (), s32[]{:S(2)}) async-start(), calls=%async_computation.2 | async-start | bytes 1114112 | tf_op jit(solution)/shard_map/all_gather | solution.py:16
  119.1 7.0 %copy-start.1 = (bf16[8,1024,1,256]{3,1,2,0:T(8,128)(2,1)S(1)}, bf16[8,1024,1,256]{3,1,2,0:T(8,128)(2,1)}, u32[]{:S(2)}) copy-start(bf16[8,1024,1,256]{3,1,2,0:T(8,128)(2,1)} %param.16) | copy-start | bytes 12582916
  129.2 223.8 %all-reduce.5.cloned.1.call-start = ((), (), s32[]{:S(2)}) async-start(), calls=%async_computation.1 | async-start | bytes 262144 | tf_op jit(solution)/shard_map/psum | solution.py:83
Sparse Core Ops, SparseCore 0:
  12.8 106.2 all-reduce.2
  129.3 55.2 all-gather.4
  230.7 122.2 all-reduce.4
where the time goes:
time: 362 us; the launch traced here: 361 us
  waiting for transfers between devices  229 us (63%)
  blocking collectives  77.6 us (21%)
  local copies, waits for them, and re-layouts  22.3 us (6%)
  between operations  13.2 us (4%)
  matrix products  12.6 us (3%)
  other arithmetic  5.93 us (2%)
    psum x1, waiting for transfers between devices, body(): return lax.psum(partial_out, ('seq', 'head'))  122 us
    psum x1, waiting for transfers between devices, body(): query = lax.psum(partial_query, 'seq')  107 us
    all_gather x2, blocking collectives, joined(): gathered = jax.tree.map(lambda a: lax.all_gather(a, axis), part)  77.6 us
    dynamic_slice x18, local copies, waits for them, and re-layouts, take(): lax.dynamic_index_in_dim(a, source, 0, False)  13.5 us
  transfers between devices with their start and end apart: 3, of which 2 were waited for; matrix products, arithmetic and copies ran while one was open for 1% of the time, Pallas kernels for 0%

commit v1 on v0

--- a/solution.py
+++ b/solution.py
@@ -51,7 +51,7 @@
     dim_rows = query_weight.shape[0]
     state_rows = lax.dynamic_slice_in_dim(hidden_state, seq_index * dim_rows, dim_rows, 1)
     partial_query = jnp.dot(state_rows, query_weight[:, 0, :], preferred_element_type=jnp.float32)
-    query = lax.psum(partial_query, "seq")
+    query = lax.all_gather(partial_query, "seq").sum(axis=0)
     query_heads = query.reshape(batch, KPG, REP, HD)
     keys_lat = latent_key[:, :, 0, :]
     values_lat = latent_value[:, :, 0, :]

time: 362 us -> 311 us (0.86)
  waiting for transfers between devices: 229 us -> 178 us
    psum x1 -> x0, waiting for transfers between devices: 107 us -> none  [body(): query = lax.psum(partial_query, 'seq')]
    all_gather x0 -> x1, waiting for transfers between devices: none -> 55.6 us  [body(): query = lax.all_gather(partial_query, 'seq').sum(axis=0)]
  transfers between devices with their start and end apart: 3 -> 3, of which waited for: 2 -> 2; matrix products, arithmetic and copies ran while one was open for 1% -> 2% of each run, Pallas kernels for 0% -> 0%
where the time goes in v1:
time: 311 us; the launch traced here: 310 us
  waiting for transfers between devices  178 us (57%)
  blocking collectives  77.3 us (25%)
  local copies, waits for them, and re-layouts  21.7 us (7%)
  between operations  13.2 us (4%)
  matrix products  12.4 us (4%)
  other arithmetic  7.2 us (2%)
    psum x1, waiting for transfers between devices, body(): return lax.psum(partial_out, ('seq', 'head'))  122 us
    all_gather x2, blocking collectives, joined(): gathered = jax.tree.map(lambda a: lax.all_gather(a, axis), part)  77.3 us
    all_gather x1, waiting for transfers between devices, body(): query = lax.all_gather(partial_query, 'seq').sum(axis=0)  55.6 us
    dynamic_slice x18, local copies, waits for them, and re-layouts, take(): lax.dynamic_index_in_dim(a, source, 0, False)  13.5 us
  transfers between devices with their start and end apart: 3, of which 2 were waited for; matrix products, arithmetic and copies ran while one was open for 2% of the time, Pallas kernels for 0%

profile of v1, /device:TPU:0, one launch (start us, length us, event | category | flops | bytes accessed | tf_op | source)
XLA Modules:
  0.0 309.9 jit_solution(14213563821367820957)
XLA Ops:
  6.5 2.2 fusion.13
  8.8 1.0 reshape.54
  9.8 1.0 reshape.55
  10.9 0.7 broadcast_compare_fusion
  11.6 0.7 compare_and_fusion
  12.4 55.6 %all-gather.7.cloned.1.call-done = f32[128,2048]{1,0:T(8,128)} async-done(((f32[8,2048]{1,0:T(8,128)}), f32[128,2048]{1,0:T(8,128)}) %all-gather.7.cloned.1.call-update) | async-done | bytes 1048592 | tf_op jit(solution)/shard_map/all_gather | solution.py:54
  67.9 1.3 bitcast_reduce_fusion
  69.3 0.4 convolution_bitcast_fusion
  69.7 5.9 %select_reduce_fusion = (f32[8,4,4]{2,1,0:T(4,128)S(1)}, f32[8,4,4,1024]{3,2,1,0:T(4,128)S(1)}) fusion(pred[8,1024]{1,0:T(8,128)(4,1)S(1)} %compare_and_fusion, f32[8,4,4,256]{3,2,1,0:T(4,128)S(1)} %convolution_bitcast_fusion, bf16[8,1024,1,256]{3,1,2,0:T(8,128)(2,1)} %param.15), kind=kOutput, calls=%fused_computation.23 | convolution fusion | flops 403046272 | bytes 4858368 | tf_op jit(solution)/shard_map/bjre,bce->bjrc/dot_general | solution.py:67
  75.6 2.1 fusion.4
  77.6 0.9 convolution_bitcast_fusion.1
  78.7 40.0 %all-gather.1 = f32[128,4,4]{2,1,0:T(4,128)S(1)} all-gather(f32[8,4,4]{2,1,0:T(4,128)S(1)} %get-tuple-element.223), channel_id=3, replica_groups=mesh['seq'=16,'head'=2] {'seq'}, dimensions={0}, use_global_device_ids=true | all-gather | bytes 8704 | tf_op jit(solution)/shard_map/all_gather | solution.py:16
  118.7 0.5 copy.36
  119.2 0.4 fusion.15
  119.6 37.3 %all-gather.2 = f32[128,4,4]{2,1,0:T(4,128)S(1)} all-gather(f32[8,4,4]{2,1,0:T(4,128)S(1)} %fusion.15), channel_id=4, replica_groups=mesh['seq'=16,'head'=2] {'seq'}, dimensions={0}, use_global_device_ids=true | all-gather | bytes 8704 | tf_op jit(solution)/shard_map/all_gather | solution.py:16
  157.1 0.5 copy.37
  157.5 0.8 slice.8
  158.4 20.1 %while.19 = (s32[]{:T(128)}, f32[8,4,4]{0,2,1:T(4,128)S(1)}, f32[8,4,4]{0,2,1:T(4,128)S(1)}, f32[8,4,4,128]{3,2,1,0:T(4,128)S(1)}, f32[16,8,4,4]{1,3,2,0:T(4,128...) while((s32[]{:T(128)}, f32[8,4,4]{0,2,1:T(4,128)S(1)}, ...), condition=%wide.region_4.5_spmd, body=%wide.region_3.4_spmd.sunk | while | flops 49925 | bytes 334991 | solution.py:21
  158.7 0.8 constant_dynamic-slice_fusion.2
  159.5 0.2 fusion.34
  160.0 0.8 constant_dynamic-slice_fusion.2
  160.8 0.2 fusion.34
  161.3 0.8 constant_dynamic-slice_fusion.2
  162.2 0.2 fusion.34
  162.7 0.8 constant_dynamic-slice_fusion.2
  163.5 0.2 fusion.34
  164.0 0.8 constant_dynamic-slice_fusion.2
  164.9 0.2 fusion.34
  165.4 0.8 constant_dynamic-slice_fusion.2
  166.2 0.2 fusion.34
  166.7 0.8 constant_dynamic-slice_fusion.2
  167.5 0.2 fusion.34
  168.0 0.8 constant_dynamic-slice_fusion.2
  168.9 0.2 fusion.34
  169.4 0.8 constant_dynamic-slice_fusion.2
  170.2 0.2 fusion.34
  170.7 0.8 constant_dynamic-slice_fusion.2
  171.6 0.2 fusion.34
  172.1 0.8 constant_dynamic-slice_fusion.2
  172.9 0.2 fusion.34
  173.4 0.8 constant_dynamic-slice_fusion.2
  174.2 0.2 fusion.34
  174.7 0.8 constant_dynamic-slice_fusion.2
  176.1 0.8 constant_dynamic-slice_fusion.2
  177.4 0.8 constant_dynamic-slice_fusion.2
  178.8 0.9 fusion.11
  179.7 122.1 %all-reduce.2.cloned.1.call-done = f32[8,4096]{1,0:T(8,128)} async-done(((f32[8,4096]{1,0:T(8,128)}), f32[8,4096]{1,0:T(8,128)}) %all-reduce.2.cloned.1.call-update) | async-done | bytes 131088 | tf_op jit(solution)/shard_map/psum | solution.py:83
  301.8 1.6 copy.82
  (70 shorter events, 5.0 us)
Async XLA Ops:
  6.5 172.2 %copy-start = (bf16[1,128,4096]{2,1,0:T(8,128)(2,1)S(1)}, bf16[1,128,4096]{2,1,0:T(8,128)(2,1)}, u32[]{:S(2)}) copy-start(bf16[1,128,4096]{2,1,0:T(8,128)(2,1)} %param.19) | copy-start | bytes 3145732
  6.5 61.4 %all-gather.7.cloned.1.call-start = ((), (), s32[]{:S(2)}) async-start(), calls=%async_computation.1 | async-start | bytes 1114112 | tf_op jit(solution)/shard_map/all_gather | solution.py:54
  8.8 148.8 %all-gather.9.cloned.1.call-start = ((), (), s32[]{:S(2)}) async-start(), calls=%async_computation.2 | async-start | bytes 1114112 | tf_op jit(solution)/shard_map/all_gather | solution.py:16
  69.3 6.3 %copy-start.1 = (bf16[8,1024,1,256]{3,1,2,0:T(8,128)(2,1)S(1)}, bf16[8,1024,1,256]{3,1,2,0:T(8,128)(2,1)}, u32[]{:S(2)}) copy-start(bf16[8,1024,1,256]{3,1,2,0:T(8,128)(2,1)} %param.16) | copy-start | bytes 12582916
  78.6 223.2 %all-reduce.2.cloned.1.call-start = ((), (), s32[]{:S(2)}) async-start(), calls=%async_computation | async-start | bytes 262144 | tf_op jit(solution)/shard_map/psum | solution.py:83
Sparse Core Ops, SparseCore 0:
  10.1 57.7 all-gather.6
  78.7 54.9 all-gather.8
  179.8 121.8 all-reduce.1

commit v2 on v0

--- a/solution.py
+++ b/solution.py
@@ -80,7 +80,8 @@
     context = (summed_all / total_all[..., None]).reshape(batch, QW).astype(jnp.bfloat16)
     context_rows = lax.dynamic_slice_in_dim(context, seq_index * out_rows, out_rows, 1)
     partial_out = jnp.dot(context_rows, out_weight[0], preferred_element_type=jnp.float32)
-    return lax.psum(partial_out, ("seq", "head"))
+    _register_core = lambda matrix: jax.lax.all_gather(matrix, ("seq", "head")).sum(axis=0)
+    return _register_core(partial_out)
 
 
 def solution(mesh):

time: 362 us -> 301 us (0.83)
  waiting for transfers between devices: 229 us -> 166 us
    psum x1 -> x0, waiting for transfers between devices: 122 us -> none  [body(): return lax.psum(partial_out, ('seq', 'head'))]
    all_gather x0 -> x1, waiting for transfers between devices: none -> 59.6 us  [body(): jax.lax.all_gather(matrix, ('seq', 'head')).sum(axis=0)]
  transfers between devices with their start and end apart: 3 -> 3, of which waited for: 2 -> 2; matrix products, arithmetic and copies ran while one was open for 1% -> 2% of each run, Pallas kernels for 0% -> 0%
where the time goes in v2:
time: 301 us; the launch traced here: 300 us
  waiting for transfers between devices  166 us (55%)
  blocking collectives  77.6 us (26%)
  local copies, waits for them, and re-layouts  20.7 us (7%)
  between operations  13.2 us (4%)
  matrix products  12.6 us (4%)
  other arithmetic  9 us (3%)
    psum x1, waiting for transfers between devices, body(): query = lax.psum(partial_query, 'seq')  107 us
    all_gather x2, blocking collectives, joined(): gathered = jax.tree.map(lambda a: lax.all_gather(a, axis), part)  77.6 us
    all_gather x1, waiting for transfers between devices, body(): jax.lax.all_gather(matrix, ('seq', 'head')).sum(axis=0)  59.6 us
    dynamic_slice x18, local copies, waits for them, and re-layouts, take(): lax.dynamic_index_in_dim(a, source, 0, False)  13.5 us
  transfers between devices with their start and end apart: 3, of which 2 were waited for; matrix products, arithmetic and copies ran while one was open for 2% of the time, Pallas kernels for 0%

profile of v2, /device:TPU:0, one launch (start us, length us, event | category | flops | bytes accessed | tf_op | source)
XLA Modules:
  0.0 299.7 jit_solution(755139538395362622)
XLA Ops:
  6.5 1.6 fusion.13
  8.1 0.7 copy.28
  8.8 0.7 broadcast_compare_fusion
  9.6 0.7 compare_and_fusion
  10.3 1.0 reshape.54
  11.4 1.0 reshape.55
  12.4 106.7 %all-reduce.2.cloned.1.call-done = f32[8,4,4,128]{3,2,1,0:T(4,128)} async-done(((f32[8,4,4,128]{3,2,1,0:T(4,128)}), f32[8,4,4,128]{3,2,1,0:T(4,128)}) %all-reduce.2.cloned.1.call-update) | async-done | bytes 65552 | tf_op jit(solution)/shard_map/psum | solution.py:54
  119.1 1.4 convolution_bitcast_fusion
  120.4 5.7 %select_reduce_fusion = (f32[8,4,4]{2,1,0:T(4,128)S(1)}, f32[8,4,4,1024]{3,2,1,0:T(4,128)S(1)}) fusion(pred[8,1024]{1,0:T(8,128)(4,1)S(1)} %compare_and_fusion, f32[8,4,4,256]{3,2,1,0:T(4,128)S(1)} %convolution_bitcast_fusion, bf16[8,1024,1,256]{3,1,2,0:T(8,128)(2,1)} %param.15), kind=kOutput, calls=%fused_computation.23 | convolution fusion | flops 403046272 | bytes 4858368 | tf_op jit(solution)/shard_map/bjre,bce->bjrc/dot_general | solution.py:67
  126.1 2.1 fusion.4
  128.2 0.9 convolution_bitcast_fusion.1
  129.2 40.4 %all-gather = f32[128,4,4]{2,1,0:T(4,128)S(1)} all-gather(f32[8,4,4]{2,1,0:T(4,128)S(1)} %get-tuple-element.223), channel_id=2, replica_groups=mesh['seq'=16,'head'=2] {'seq'}, dimensions={0}, use_global_device_ids=true | all-gather | bytes 8704 | tf_op jit(solution)/shard_map/all_gather | solution.py:16
  169.8 0.5 copy.37
  170.2 0.4 fusion.15
  170.6 37.1 %all-gather.1 = f32[128,4,4]{2,1,0:T(4,128)S(1)} all-gather(f32[8,4,4]{2,1,0:T(4,128)S(1)} %fusion.15), channel_id=3, replica_groups=mesh['seq'=16,'head'=2] {'seq'}, dimensions={0}, use_global_device_ids=true | all-gather | bytes 8704 | tf_op jit(solution)/shard_map/all_gather | solution.py:16
  207.9 0.5 copy.38
  208.4 0.8 slice.8
  209.2 20.1 %while.19 = (s32[]{:T(128)}, f32[8,4,4]{0,2,1:T(4,128)S(1)}, f32[8,4,4]{0,2,1:T(4,128)S(1)}, f32[8,4,4,128]{3,2,1,0:T(4,128)S(1)}, f32[16,8,4,4]{1,3,2,0:T(4,128...) while((s32[]{:T(128)}, f32[8,4,4]{0,2,1:T(4,128)S(1)}, ...), condition=%wide.region_4.5_spmd, body=%wide.region_3.4_spmd.sunk | while | flops 49925 | bytes 334991 | solution.py:21
  209.5 0.8 constant_dynamic-slice_fusion.2
  210.3 0.2 fusion.34
  210.8 0.8 constant_dynamic-slice_fusion.2
  211.7 0.2 fusion.34
  212.2 0.8 constant_dynamic-slice_fusion.2
  213.0 0.2 fusion.34
  213.5 0.8 constant_dynamic-slice_fusion.2
  214.4 0.2 fusion.34
  214.9 0.8 constant_dynamic-slice_fusion.2
  215.7 0.2 fusion.34
  216.2 0.8 constant_dynamic-slice_fusion.2
  217.0 0.2 fusion.34
  217.5 0.8 constant_dynamic-slice_fusion.2
  218.4 0.2 fusion.34
  218.9 0.8 constant_dynamic-slice_fusion.2
  219.7 0.2 fusion.34
  220.2 0.8 constant_dynamic-slice_fusion.2
  221.1 0.2 fusion.34
  221.5 0.8 constant_dynamic-slice_fusion.2
  222.9 0.8 constant_dynamic-slice_fusion.2
  224.2 0.8 constant_dynamic-slice_fusion.2
  225.1 0.2 fusion.34
  225.6 0.8 constant_dynamic-slice_fusion.2
  226.4 0.2 fusion.34
  226.9 0.8 constant_dynamic-slice_fusion.2
  228.2 0.8 constant_dynamic-slice_fusion.2
  229.1 0.2 fusion.34
  229.6 0.9 fusion.11
  230.5 59.6 %all-gather.9.cloned.1.call-done = f32[256,4096]{1,0:T(8,128)} async-done(((f32[8,4096]{1,0:T(8,128)}), f32[256,4096]{1,0:T(8,128)}) %all-gather.9.cloned.1.call-update) | async-done | bytes 4194320 | tf_op jit(solution)/shard_map/all_gather | solution.py:83
  290.1 3.0 %bitcast_reduce_fusion = f32[8,4096]{1,0:T(8,128)} fusion(f32[256,4096]{1,0:T(8,128)} %all-gather.9.cloned.1.call-done), kind=kLoop, calls=%fused_computation.14 | loop fusion | flops 1015808 | bytes 4325376 | tf_op jit(solution)/shard_map/reduce_sum | solution.py:83
  (69 shorter events, 5.0 us)
Async XLA Ops:
  6.5 223.1 %copy-start = (bf16[1,128,4096]{2,1,0:T(8,128)(2,1)S(1)}, bf16[1,128,4096]{2,1,0:T(8,128)(2,1)}, u32[]{:S(2)}) copy-start(bf16[1,128,4096]{2,1,0:T(8,128)(2,1)} %param.19) | copy-start | bytes 3145732
  6.5 112.5 %all-reduce.2.cloned.1.call-start = ((), (), s32[]{:S(2)}) async-start(), calls=%async_computation | async-start | bytes 131072 | tf_op jit(solution)/shard_map/psum | solution.py:54
  8.8 199.6 %all-gather.7.cloned.1.call-start = ((), (), s32[]{:S(2)}) async-start(), calls=%async_computation.1 | async-start | bytes 1114112 | tf_op jit(solution)/shard_map/all_gather | solution.py:16
  119.1 7.0 %copy-start.1 = (bf16[8,1024,1,256]{3,1,2,0:T(8,128)(2,1)S(1)}, bf16[8,1024,1,256]{3,1,2,0:T(8,128)(2,1)}, u32[]{:S(2)}) copy-start(bf16[8,1024,1,256]{3,1,2,0:T(8,128)(2,1)} %param.16) | copy-start | bytes 12582916
  129.2 161.0 %all-gather.9.cloned.1.call-start = ((), (), s32[]{:S(2)}) async-start(), calls=%async_computation.2 | async-start | bytes 4325376 | tf_op jit(solution)/shard_map/all_gather | solution.py:83
Sparse Core Ops, SparseCore 0:
  12.8 106.2 all-reduce.1
  129.3 55.2 all-gather.6
  230.7 59.4 all-gather.8
